TPU v7x, 32 devices: a whole 2x2x4 slice. The times are simulated.
32 devices in a mesh: row: 4 (over z), col: 2 (over y), layer: 4 (over x, core).
Axes of the slice: x: 2, y: 2, z: 4, core: 2. Of those that a mesh axis runs over, the one named last changes fastest.
Arguments:
- tokens: bfloat16 [1280, 6144], P('row', 'layer'), may hold values from -6 to 6
- expert_ids: int32 [1280, 2], replicated, may hold values from 0 to 7, all different within a row; in each aligned block of 1280 rows (0 to 1279, 1280 to 2559, ...) at most 640 rows name the same one
- w_gate: bfloat16 [2, 6144, 8192], P(None, 'layer', ('row', 'col')), may hold values from -0.078125 to 0.078125
- w_up: bfloat16 [2, 6144, 8192], P(None, 'layer', ('row', 'col')), may hold values from -0.078125 to 0.078125
Outputs:
- hidden: bfloat16 [2, 640, 8192], P(None, ('col', 'layer'), 'row')
Inputs may be any that keep to these rules, and one draw needn't show every extreme that they name: `expert_ids`: each token names 2 different experts. No expert is named by more than 640 tokens, a bound that some block reaches.
All inputs are finite; a program needn't handle non-finite values.
Results may differ from a plain program's by a relative error of at most 0.0012.
Values may be sent and summed in bfloat16 or wider, within the bound.
A program may use at most 128 MiB of HBM per device.

v0:
```python
import jax
import jax.numpy as jnp
from jax import lax
from jax.sharding import PartitionSpec as P

SLOTS_DEV = 80


def passed_along(value, axis, steps):
    count = lax.axis_size(axis)
    pairs = [(source, (source + steps) % count) for source in range(count)]
    return lax.ppermute(value, axis, pairs)


def shards(tokens, expert_ids, w_gate, w_up):
    col_count = lax.axis_size("col")
    layer_count = lax.axis_size("layer")
    row_count = lax.axis_size("row")
    col_index = lax.axis_index("col")
    row_index = lax.axis_index("row")
    experts = w_gate.shape[0]
    capacity = SLOTS_DEV * col_count * layer_count
    slot_block = capacity // col_count
    local_rows = tokens.shape[0]
    tok_count = local_rows * row_count
    expert_range = jnp.arange(experts, dtype=jnp.int32)
    member = jnp.any(expert_ids[:, :, None] == expert_range[None, None, :], axis=1).astype(
        jnp.int32
    )
    slot_rank = jnp.cumsum(member, axis=0) - member
    target = jnp.where(member > 0, slot_rank, capacity)
    token_range = jnp.broadcast_to(jnp.arange(tok_count, dtype=jnp.int32)[:, None], target.shape)
    slot_table = (
        jnp.zeros((experts, capacity + 1), jnp.int32)
        .at[expert_range[None, :], target]
        .set(token_range)
    )
    counts = jnp.sum(member, axis=0)
    slot_start = col_index * slot_block
    picked = lax.dynamic_slice_in_dim(slot_table, slot_start, slot_block, 1)
    position = slot_start + jnp.arange(slot_block, dtype=jnp.int32)
    live_mask = position[None, :] < counts[:, None]
    row_start = row_index * local_rows
    local_pick = picked - row_start
    inside = live_mask & (local_pick >= 0) & (local_pick < local_rows)
    own_rows = tokens[jnp.clip(local_pick, 0, local_rows - 1)]
    placed = jnp.where(inside[:, :, None], own_rows, jnp.zeros((), tokens.dtype)).astype(
        jnp.float32
    )
    slot_rows = lax.psum(placed.astype(jnp.bfloat16), "row")
    stacked = jnp.stack((w_gate, w_up))
    narrow = w_gate.shape[2]
    totals = jnp.zeros((2, experts, slot_block, narrow * col_count), jnp.float32)
    moving = stacked
    for step in range(col_count):
        which_block = (col_index - step) % col_count
        totals = lax.dynamic_update_slice_in_dim(
            totals,
            jnp.einsum("ecd,pedf->pecf", slot_rows, moving, preferred_element_type=jnp.float32),
            which_block * narrow,
            3,
        )
        if step + 1 < col_count:
            moving = passed_along(moving, "col", 1)
    parts = lax.psum_scatter(totals, "layer", scatter_dimension=2, tiled=True)
    return (jax.nn.silu(parts[0]) * parts[1]).astype(jnp.bfloat16)


def solution(mesh):
    in_specs = (
        P("row", "layer"),
        P(),
        P(None, "layer", ("row", "col")),
        P(None, "layer", ("row", "col")),
    )
    out_specs = P(None, ("col", "layer"), "row")
    return jax.shard_map(shards, mesh=mesh, in_specs=in_specs, out_specs=out_specs, check_vma=False)
```

profile of v0, /device:TPU:0, one launch (start us, length us, event | category | flops | bytes accessed | tf_op | source)
XLA Modules:
  0.0 396.8 jit_solution(5306595772369583344)
XLA Ops:
  6.5 0.0 copy-start.4
  6.6 10.5 %pad_maximum_fusion = bf16[2,2,1536,1024]{3,2,0,1:T(8,128)(2,1)} fusion(bf16[1,2,1536,1024]{3,2,0,1:T(8,128)(2,1)} %bitcast.45, bf16[1,2,1536,1024]{3,2,0,1:T(8,128)(2,1)} %bitcast.47), kind=kLoop, calls=%fused_computation.2 | loop fusion | flops 6291456 | bytes 25165824 | tf_op jit(solution)/shard_map/stack | solution.py:51
  17.0 3.0 collective-permute-start
  20.1 0.6 reduce-window.6
  20.7 0.2 slice_reduce_fusion
  20.9 0.2 reduce-window.9
  21.1 0.1 add_bitcast_fusion
  21.1 0.1 convert_reduce_fusion
  21.3 0.1 multiply_reduce_fusion
  21.4 0.1 and_reduce_fusion
  21.5 0.3 copy.15
  21.8 0.3 reshape.36
  22.1 0.3 reshape.38
  22.5 9.9 %scatter_custom_fusion = s32[1282]{0:T(1024)S(1)} fusion(s32[2560]{0:T(1024)S(1)} %reshape.36, s32[2560]{0:T(1024)S(1)} %reshape.38, s32[]{:T(128)} %constant.28.clone.1), kind=kCustom, calls=%fused_computation.31 | custom fusion | bytes 5132
  32.4 0.1 reshape.26
  32.5 0.1 compare_select_fusion.2
  32.5 0.1 reshape.30
  32.6 3.1 gather_fusion
  35.7 0.1 compare_and_fusion
  35.8 1.6 broadcast_select_fusion
  37.4 0.0 all-reduce.2.cloned.1.call-update
  37.4 0.0 reduce-scatter.2.cloned.1.call-start
  37.5 82.2 %all-reduce.2.cloned.1.call-done = bf16[2,320,1536]{2,1,0:T(8,128)(2,1)} async-done(((bf16[2,320,1536]{2,1,0:T(8,128)(2,1)}), bf16[2,320,1536]{2,1,0:T(8,128)(2,1)}) %all-reduce.2.cloned.1.call-update) | async-done | bytes 1966096 | tf_op jit(solution)/shard_map/psum | solution.py:50
  119.7 7.9 %convolution_bitcast_fusion.1 = f32[2,2,320,1024]{3,2,0,1:T(8,128)S(1)} fusion(bf16[2,320,1536]{2,1,0:T(8,128)(2,1)} %all-reduce.2.cloned.1.call-done, bf16[1,2,1536,1024]{3,2,0,1:T(8,128)(2,1)} %bitcast.46, bf16[1,2,1536,1024]{3,2,0,1:T(8,128)(2,1)} %bitcast.48), kind=kOutput, calls=%fused_computation.6 | convolution fusion | flops 4051697664 | bytes 19791872 | tf_op jit(solution)/shard_map/ecd,pedf->pecf/dot_general | solution.py:59
  127.6 5.2 %broadcast_in_dim.45 = f32[2,2,320,2048]{3,2,1,0:T(8,128)} broadcast(f32[]{:T(128)} %constant.20.clone.1), dimensions={} | broadcast | bytes 10485764 | tf_op jit(solution)/shard_map/broadcast_in_dim | solution.py:53
  132.8 2.7 copy_dynamic-update-slice_fusion.1
  135.5 155.2 %collective-permute-done = bf16[2,2,1536,1024]{3,2,0,1:T(8,128)(2,1)} collective-permute-done((bf16[2,2,1536,1024]{3,2,0,1:T(8,128)(2,1)}, bf16[2,2,1536,1024]{3,2,0,1:T(8,128)(2,1)}, u32[]{:S(2)}, u32[]{:S(2)}) %collective-permute-start) | collective-permute-done | bytes 12582944 | tf_op jit(solution)/shard_map/ppermute | solution.py:12
  290.7 7.4 %convolution_bitcast_fusion = f32[2,2,320,1024]{3,2,0,1:T(8,128)S(1)} fusion(bf16[2,2,1536,1024]{3,2,0,1:T(8,128)(2,1)} %collective-permute-done, bf16[2,320,1536]{2,1,0:T(8,128)(2,1)S(1)} %copy-done.5), kind=kOutput, calls=%fused_computation.5 | convolution fusion | flops 4026531840 | bytes 19791872 | tf_op jit(solution)/shard_map/ecd,pedf->pecf/dot_general | solution.py:59
  298.1 3.0 copy_dynamic-update-slice_fusion
  301.1 0.0 reduce-scatter.2.cloned.1.call-update
  301.1 86.0 %reduce-scatter.2.cloned.1.call-done = f32[2,2,80,2048]{3,2,1,0:T(8,128)} async-done(((f32[2,2,320,2048]{3,2,1,0:T(8,128)}), f32[2,2,80,2048]{3,2,1,0:T(8,128)}) %reduce-scatter.2.cloned.1.call-update) | async-done | bytes 2621456 | tf_op jit(solution)/shard_map/reduce_scatter | solution.py:65
  387.1 2.9 fusion.3
  (20 shorter events, 0.1 us)
Async XLA Ops:
  6.5 26.1 %copy-start = (bf16[320,1536]{1,0:T(8,128)(2,1)S(1)}, bf16[320,1536]{1,0:T(8,128)(2,1)}, u32[]{:S(2)}) copy-start(bf16[320,1536]{1,0:T(8,128)(2,1)} %param.4) | copy-start | bytes 2949124
  6.5 113.2 %all-reduce.2.cloned.1.call-start = ((), (), s32[]{:S(2)}) async-start(), calls=%async_computation.1 | async-start | bytes 3932160 | tf_op jit(solution)/shard_map/psum | solution.py:50
  6.5 13.5 %copy-start.2 = (s32[1280,2]{0,1:T(2,128)S(1)}, s32[1280,2]{0,1:T(2,128)}, u32[]{:S(2)}) copy-start(s32[1280,2]{0,1:T(2,128)} %param.5) | copy-start | bytes 30724
  6.5 14.7 %copy-start.3 = (s32[2]{0:T(128)S(1)}, s32[2]{0:T(128)}, u32[]{:S(2)}) copy-start(s32[2]{0:T(128)} %constant.63) | copy-start | bytes 28
  6.5 14.8 %copy-start.4 = (s32[2]{0:T(128)S(1)}, s32[2]{0:T(128)}, u32[]{:S(2)}) copy-start(s32[2]{0:T(128)} %constant.66) | copy-start | bytes 28
  17.0 273.6 %collective-permute-start = (bf16[2,2,1536,1024]{3,2,0,1:T(8,128)(2,1)}, bf16[2,2,1536,1024]{3,2,0,1:T(8,128)(2,1)}, u32[]{:S(2)}, u32[]{:S(2)}) collective-permute-start(bf16[2,2,1536,1024]{3,2,0,1:T(8,128)(2,1)} %pad_maximum_fusion), channel_id=1, source_target_pairs={{0,4},{4,0},{1,5},{5,1},{2,6},{6,2},{3,7},{7,3},{8,12},{12,8},{9,1... | collective-permute-start | bytes 37748744 | tf_op jit(solution)/shard_map/ppermute | solution.py:12
  37.4 349.6 %reduce-scatter.2.cloned.1.call-start = ((), (), s32[]{:S(2)}) async-start(), calls=%async_computation.2 | async-start | bytes 13107200 | tf_op jit(solution)/shard_map/reduce_scatter | solution.py:65
  132.8 157.9 %copy-start.5 = (bf16[2,320,1536]{2,1,0:T(8,128)(2,1)S(1)}, bf16[2,320,1536]{2,1,0:T(8,128)(2,1)}, u32[]{:S(2)}) copy-start(bf16[2,320,1536]{2,1,0:T(8,128)(2,1)} %all-reduce.2.cloned.1.call-done) | copy-start | bytes 5898244
  301.1 88.9 %copy-start.1 = (bf16[320,1536]{1,0:T(8,128)(2,1)S(1)}, bf16[320,1536]{1,0:T(8,128)(2,1)}, u32[]{:S(2)}) copy-start(bf16[320,1536]{1,0:T(8,128)(2,1)} %param.4) | copy-start | bytes 2949124
Sparse Core Ops, SparseCore 0:
  37.5 82.1 all-reduce.1
  301.2 85.7 reduce-scatter.1
where the time goes:
time: 397 us
  waiting for transfers between devices  323 us (81%)
  local copies, waits for them, and re-layouts  25.2 us (6%)
  other arithmetic  16.3 us (4%)
  matrix products  15.3 us (4%)
  between operations  13.6 us (3%)
    ppermute x1, waiting for transfers between devices, passed_along(): return lax.ppermute(value, axis, pairs)  155 us
    reduce_scatter x1, waiting for transfers between devices, shards(): parts = lax.psum_scatter(totals, 'layer', scatter_dimension=2, tiled=True)  86 us
    psum x1, waiting for transfers between devices, shards(): slot_rows = lax.psum(placed.astype(jnp.bfloat16), 'row')  82.2 us
    dot_general x2, matrix products, shards(): jnp.einsum('ecd,pedf->pecf', slot_rows, moving, preferred_element_type=jn...  15.3 us
    unnamed x15, local copies, waits for them, and re-layouts  10.5 us
    another operation x1, other arithmetic, shards(): stacked = jnp.stack((w_gate, w_up))  10.5 us
  transfers between devices with their start and end apart: 3, of which 3 were waited for; matrix products, arithmetic and copies ran while one was open for 8% of the time, Pallas kernels for 0%

commit v1 on v0

--- a/solution.py
+++ b/solution.py
@@ -47,7 +47,7 @@
     placed = jnp.where(inside[:, :, None], own_rows, jnp.zeros((), tokens.dtype)).astype(
         jnp.float32
     )
-    slot_rows = lax.psum(placed.astype(jnp.bfloat16), "row")
+    slot_rows = jnp.sum(lax.all_gather(placed.astype(jnp.bfloat16), "row"), axis=0)
     stacked = jnp.stack((w_gate, w_up))
     narrow = w_gate.shape[2]
     totals = jnp.zeros((2, experts, slot_block, narrow * col_count), jnp.float32)

time: 397 us -> 416 us (1.048)
  waiting for transfers between devices: 323 us -> 336 us
  other arithmetic: 16.3 us -> 23.4 us
    all_gather x0 -> x1, waiting for transfers between devices: none -> 130 us  [shards(): lax.all_gather(placed.astype(jnp.bfloat16), 'row')]
    psum x1 -> x0, waiting for transfers between devices: 82.2 us -> none  [shards(): slot_rows = lax.psum(placed.astype(jnp.bfloat16), 'row')]
    ppermute x1, waiting for transfers between devices: 155 us -> 120 us  [passed_along(): return lax.ppermute(value, axis, pairs)]
    reduce_sum x0 -> x1, other arithmetic: none -> 5.1 us  [shards(): jnp.sum(lax.all_gather(placed.astype(jnp.bfloat16), 'row'), axis=0)]
    unnamed x15 -> x7, local copies, waits for them, and re-layouts: 10.5 us -> 10.5 us
  transfers between devices with their start and end apart: 3 -> 3, of which waited for: 3 -> 3; matrix products, arithmetic and copies ran while one was open for 8% -> 7% of each run, Pallas kernels for 0% -> 0%
where the time goes in v1:
time: 416 us
  waiting for transfers between devices  336 us (81%)
  local copies, waits for them, and re-layouts  25.2 us (6%)
  other arithmetic  23.4 us (6%)
  matrix products  14.5 us (3%)
  between operations  13.5 us (3%)
    all_gather x1, waiting for transfers between devices, shards(): lax.all_gather(placed.astype(jnp.bfloat16), 'row')  130 us
    ppermute x1, waiting for transfers between devices, passed_along(): return lax.ppermute(value, axis, pairs)  120 us
    reduce_scatter x1, waiting for transfers between devices, shards(): parts = lax.psum_scatter(totals, 'layer', scatter_dimension=2, tiled=True)  86 us
    dot_general x2, matrix products, shards(): jnp.einsum('ecd,pedf->pecf', slot_rows, moving, preferred_element_type=jn...  14.5 us
    unnamed x7, local copies, waits for them, and re-layouts  10.5 us
    another operation x1, other arithmetic, shards(): stacked = jnp.stack((w_gate, w_up))  10.5 us
  transfers between devices with their start and end apart: 3, of which 3 were waited for; matrix products, arithmetic and copies ran while one was open for 7% of the time, Pallas kernels for 0%

profile of v1, /device:TPU:0, one launch (start us, length us, event | category | flops | bytes accessed | tf_op | source)
XLA Modules:
  0.0 416.1 jit_solution(274157988476845334)
XLA Ops:
  6.5 0.8 compare_reduce_fusion
  7.4 0.6 reduce-window.6
  8.0 0.2 slice_reduce_fusion
  8.2 0.2 reduce-window.9
  8.3 0.1 add_bitcast_fusion
  8.4 0.1 convert_reduce_fusion
  8.6 0.8 and_reduce_fusion
  9.3 0.7 multiply_reduce_fusion
  10.1 0.3 copy.15
  10.4 0.3 reshape.43
  10.7 0.3 reshape.45
  11.1 9.9 %scatter_custom_fusion = s32[1282]{0:T(1024)S(1)} fusion(s32[2560]{0:T(1024)S(1)} %reshape.43, s32[2560]{0:T(1024)S(1)} %reshape.45, s32[]{:T(128)} %constant.29.clone.1), kind=kCustom, calls=%fused_computation.31 | custom fusion | bytes 5132
  21.0 0.1 reshape.33
  21.1 0.1 compare_select_fusion.2
  21.1 0.1 reshape.37
  21.2 0.1 compare_and_fusion
  21.3 3.1 gather_fusion
  24.4 1.5 broadcast_select_fusion
  25.9 0.0 reduce-scatter.2.cloned.1.call-start
  26.0 10.5 %pad_maximum_fusion = bf16[2,2,1536,1024]{3,2,0,1:T(8,128)(2,1)} fusion(bf16[1,2,1536,1024]{3,2,0,1:T(8,128)(2,1)} %bitcast.46, bf16[1,2,1536,1024]{3,2,0,1:T(8,128)(2,1)} %bitcast.48), kind=kLoop, calls=%fused_computation.2 | loop fusion | flops 6291456 | bytes 25165824 | tf_op jit(solution)/shard_map/stack | solution.py:51
  36.4 3.2 collective-permute-start
  39.6 130.2 %all-gather.2.cloned.1.call-done = bf16[4,2,320,1536]{3,2,1,0:T(8,128)(2,1)} async-done(((bf16[1,2,320,1536]{3,2,1,0:T(8,128)(2,1)}), bf16[4,2,320,1536]{3,2,1,0:T(8,128)(2,1)}) %all-gather.2.cloned.1.call-update) | async-done | bytes 7864336 | tf_op jit(solution)/shard_map/all_gather | solution.py:50
  169.8 5.1 %reduce_sum.22 = bf16[2,320,1536]{2,1,0:T(8,128)(2,1)S(1)} reduce(bf16[4,2,320,1536]{3,2,1,0:T(8,128)(2,1)} %all-gather.2.cloned.1.call-done, bf16[]{:T(256)} %constant.58.clone.1), dimensions={0}, to_apply=%region_5.6 | reduce | flops 2949120 | bytes 9830402 | tf_op jit(solution)/shard_map/reduce_sum | solution.py:50
  175.0 7.3 %convolution_bitcast_fusion.1 = f32[2,2,320,1024]{3,2,0,1:T(8,128)S(1)} fusion(bf16[2,320,1536]{2,1,0:T(8,128)(2,1)S(1)} %reduce_sum.22, bf16[1,2,1536,1024]{3,2,0,1:T(8,128)(2,1)} %bitcast.47, bf16[1,2,1536,1024]{3,2,0,1:T(8,128)(2,1)} %bitcast.49), kind=kOutput, calls=%fused_computation.6 | convolution fusion | flops 4051697664 | bytes 19791872 | tf_op jit(solution)/shard_map/ecd,pedf->pecf/dot_general | solution.py:59
  182.2 5.2 %broadcast_in_dim.45 = f32[2,2,320,2048]{3,2,1,0:T(8,128)} broadcast(f32[]{:T(128)} %constant.21.clone.1), dimensions={} | broadcast | bytes 10485764 | tf_op jit(solution)/shard_map/broadcast_in_dim | solution.py:53
  187.5 2.7 copy_dynamic-update-slice_fusion.1
  190.1 120.1 %collective-permute-done = bf16[2,2,1536,1024]{3,2,0,1:T(8,128)(2,1)} collective-permute-done((bf16[2,2,1536,1024]{3,2,0,1:T(8,128)(2,1)}, bf16[2,2,1536,1024]{3,2,0,1:T(8,128)(2,1)}, u32[]{:S(2)}, u32[]{:S(2)}) %collective-permute-start) | collective-permute-done | bytes 12582944 | tf_op jit(solution)/shard_map/ppermute | solution.py:12
  310.2 7.2 %convolution_bitcast_fusion = f32[2,2,320,1024]{3,2,0,1:T(8,128)S(1)} fusion(bf16[2,2,1536,1024]{3,2,0,1:T(8,128)(2,1)} %collective-permute-done, bf16[2,320,1536]{2,1,0:T(8,128)(2,1)S(1)} %reduce_sum.22), kind=kOutput, calls=%fused_computation.5 | convolution fusion | flops 4026531840 | bytes 19791872 | tf_op jit(solution)/shard_map/ecd,pedf->pecf/dot_general | solution.py:59
  317.4 3.0 copy_dynamic-update-slice_fusion
  320.4 0.0 reduce-scatter.2.cloned.1.call-update
  320.4 86.0 %reduce-scatter.2.cloned.1.call-done = f32[2,2,80,2048]{3,2,1,0:T(8,128)} async-done(((f32[2,2,320,2048]{3,2,1,0:T(8,128)}), f32[2,2,80,2048]{3,2,1,0:T(8,128)}) %reduce-scatter.2.cloned.1.call-update) | async-done | bytes 2621456 | tf_op jit(solution)/shard_map/reduce_scatter | solution.py:65
  406.4 2.9 fusion.3
  (13 shorter events, 0.1 us)
Async XLA Ops:
  6.5 14.8 %copy-start = (bf16[320,1536]{1,0:T(8,128)(2,1)S(1)}, bf16[320,1536]{1,0:T(8,128)(2,1)}, u32[]{:S(2)}) copy-start(bf16[320,1536]{1,0:T(8,128)(2,1)} %param.4) | copy-start | bytes 2949124
  6.5 163.3 %all-gather.2.cloned.1.call-start = ((), (), s32[]{:S(2)}) async-start(), calls=%async_computation.1 | async-start | bytes 9830400 | tf_op jit(solution)/shard_map/all_gather | solution.py:50
  25.9 380.5 %reduce-scatter.2.cloned.1.call-start = ((), (), s32[]{:S(2)}) async-start(), calls=%async_computation.2 | async-start | bytes 13107200 | tf_op jit(solution)/shard_map/reduce_scatter | solution.py:65
  36.4 273.8 %collective-permute-start = (bf16[2,2,1536,1024]{3,2,0,1:T(8,128)(2,1)}, bf16[2,2,1536,1024]{3,2,0,1:T(8,128)(2,1)}, u32[]{:S(2)}, u32[]{:S(2)}) collective-permute-start(bf16[2,2,1536,1024]{3,2,0,1:T(8,128)(2,1)} %pad_maximum_fusion), channel_id=1, source_target_pairs={{0,4},{4,0},{1,5},{5,1},{2,6},{6,2},{3,7},{7,3},{8,12},{12,8},{9,1... | collective-permute-start | bytes 37748744 | tf_op jit(solution)/shard_map/ppermute | solution.py:12
  320.4 89.0 %copy-start.1 = (bf16[320,1536]{1,0:T(8,128)(2,1)S(1)}, bf16[320,1536]{1,0:T(8,128)(2,1)}, u32[]{:S(2)}) copy-start(bf16[320,1536]{1,0:T(8,128)(2,1)} %param.4) | copy-start | bytes 2949124
Sparse Core Ops, SparseCore 0:
  26.0 143.7 all-gather.1
  320.5 85.8 reduce-scatter.1
